TPU v7x, 32 devices: a whole 2x2x4 slice. The times are simulated.
32 devices in a mesh: dp: 8 (over z, y), seq: 4 (over x, core).
Axes of the slice: x: 2, y: 2, z: 4, core: 2. Of those that a mesh axis runs over, the one named last changes fastest.
Arguments:
- byte_states: bfloat16 [8, 1024, 1024], P('dp', 'seq'), may hold values from -6 to 6
- kv_weight: bfloat16 [1024, 1024], P('dp'), may hold values from -0.1875 to 0.1875
- patch_query: bfloat16 [8, 256, 512], P('dp', 'seq'), may hold values from -96 to 96
- out_grad: bfloat16 [8, 256, 512], P('dp', 'seq'), may hold values from -3 to 3
- patch_start: int32 [8, 4, 64], P('dp'), may hold values from 0 to 256, as said below
- patch_count: int32 [8, 4], P('dp'), may hold values from 16 to 64, as said below
Outputs:
- byte_grad: bfloat16 [8, 1024, 1024], P('dp', 'seq')
- query_grad: bfloat16 [8, 256, 512], P('dp', 'seq')
- kv_grad: float32 [1024, 1024], P('dp', 'seq')
Inputs may be any that keep to these rules, and one draw needn't show every extreme that they name: `patch_start`: within a shard the live starts rise strictly; the first start is below 64 and equals 63 in some shard; slots from patch_count on hold 256. `patch_count`: some shard holds 64 patches.
All inputs are finite; a program needn't handle non-finite values.
Results may differ from a plain program's by a relative error of at most 0.03.
Values may be sent and summed in bfloat16 or wider, within the bound.
A program may use at most 64 MiB of HBM per device.

v0:
```python
import functools
import math

import jax
import jax.numpy as jnp
from jax import lax
from jax.experimental import pallas as pl
from jax.experimental.pallas import tpu as pltpu
from jax.sharding import PartitionSpec as P

HEADS = 8
HD = 64
PSLOT = 64
REACH = 64


def from_behind(value, axis, steps):
    count = lax.axis_size(axis)
    initial, last = (max(0, -steps), min(count, count - steps))
    return lax.ppermute(value, axis, [(source, source + steps) for source in range(initial, last)])


def plain_body(byte_states, kv_weight, patch_query, out_grad, patch_start, patch_count):
    seq_here, own_bytes, model_width = byte_states.shape
    half_width = patch_query.shape[2]
    shards = lax.axis_size("seq")
    position = lax.axis_index("seq")
    attn_scale = 1.0 / math.sqrt(HD)
    highest = lax.Precision.HIGHEST
    weight = lax.all_gather(kv_weight, "dp", axis=0, tiled=True)
    counts_here = lax.dynamic_slice_in_dim(patch_count, position, 1, 1)[:, 0]
    live_total = lax.psum(jnp.sum(counts_here.astype(jnp.float32)), ("dp", "seq"))
    loss_scale = jnp.float32(seq_here * lax.axis_size("dp") * shards * PSLOT) / live_total
    borrowed = from_behind(byte_states[:, :REACH], "seq", -1)
    extended = jnp.concatenate([byte_states, borrowed], 1)
    ext_rows = extended.shape[1]
    flat_states = extended.reshape(seq_here * ext_rows, model_width)
    projected = jnp.dot(flat_states, weight, preferred_element_type=jnp.float32).astype(
        jnp.bfloat16
    )
    projected = projected.reshape(seq_here, ext_rows, 2 * half_width)
    key_rows = (
        projected[..., :half_width].reshape(seq_here, ext_rows, HEADS, HD).astype(jnp.float32)
    )
    value_rows = (
        projected[..., half_width:].reshape(seq_here, ext_rows, HEADS, HD).astype(jnp.float32)
    )
    starts_here = lax.dynamic_slice_in_dim(patch_start, position, 1, 1)[:, 0, :]
    next_shard = jnp.minimum(position + 1, shards - 1)
    next_first = lax.dynamic_slice_in_dim(patch_start, next_shard, 1, 1)[:, 0, 0]
    final_end = jnp.where(position < shards - 1, own_bytes + next_first, own_bytes)
    slot_ids = jnp.arange(PSLOT, dtype=jnp.int32)
    shifted = jnp.concatenate([starts_here[:, 1:], starts_here[:, :1]], 1)
    patch_end = jnp.where(slot_ids[None, :] + 1 < counts_here[:, None], shifted, final_end[:, None])
    live_slots = slot_ids[None, :] < counts_here[:, None]
    byte_pos = jnp.arange(ext_rows, dtype=jnp.int32)
    member = (
        (byte_pos[None, :, None] >= starts_here[:, None, :])
        & (byte_pos[None, :, None] < patch_end[:, None, :])
        & live_slots[:, None, :]
    )
    inside = jnp.any(member, axis=2)
    onehot = member.astype(jnp.bfloat16)
    onehot_float = member.astype(jnp.float32)
    paired = jnp.concatenate([patch_query, out_grad], 2)
    spread = jnp.einsum("stp,spc->stc", onehot, paired, preferred_element_type=jnp.float32)
    query_rows = spread[..., :half_width].reshape(seq_here, ext_rows, HEADS, HD)
    upstream = spread[..., half_width:].reshape(seq_here, ext_rows, HEADS, HD)
    scores = jnp.sum(query_rows * key_rows, -1) * attn_scale
    masked = jnp.where(member[..., None], scores[:, :, None, :], -jnp.inf)
    row_peak = jnp.where(live_slots[..., None], jnp.max(masked, axis=1), 0.0)
    peak_rows = jnp.einsum("stp,sph->sth", onehot_float, row_peak, precision=highest)
    exponent = jnp.where(inside[..., None], jnp.exp(scores - peak_rows), 0.0)
    denominator = jnp.einsum("stp,sth->sph", onehot_float, exponent, precision=highest)
    denominator = jnp.where(live_slots[..., None], denominator, 1.0)
    denom_rows = jnp.einsum("stp,sph->sth", onehot_float, denominator, precision=highest)
    denom_rows = jnp.where(inside[..., None], denom_rows, 1.0)
    probabilities = exponent / denom_rows
    prob_half = lax.optimization_barrier(probabilities.astype(jnp.bfloat16)).astype(jnp.float32)
    prob_grad = jnp.sum(upstream * value_rows, -1)
    delta_sum = jnp.einsum(
        "stp,sth->sph", onehot_float, probabilities * prob_grad, precision=highest
    )
    delta_rows = jnp.einsum("stp,sph->sth", onehot_float, delta_sum, precision=highest)
    score_grad = (probabilities * (prob_grad - delta_rows) * attn_scale).astype(jnp.bfloat16)
    score_grad = lax.optimization_barrier(score_grad).astype(jnp.float32)
    weighted_keys = (score_grad[..., None] * key_rows).reshape(seq_here, ext_rows, half_width)
    query_grad = jnp.einsum("stp,stc->spc", onehot_float, weighted_keys, precision=highest)
    query_grad = (loss_scale * query_grad).astype(jnp.bfloat16)
    key_grad = (loss_scale * score_grad[..., None] * query_rows).reshape(
        seq_here, ext_rows, half_width
    )
    value_grad = (loss_scale * prob_half[..., None] * upstream).reshape(
        seq_here, ext_rows, half_width
    )
    proj_grad = jnp.concatenate([key_grad, value_grad], 2).astype(jnp.bfloat16)
    flat_grads = proj_grad.reshape(seq_here * ext_rows, 2 * half_width)
    state_grad = lax.dot_general(
        flat_grads, weight, (((1,), (1,)), ((), ())), preferred_element_type=jnp.float32
    )
    state_grad = state_grad.reshape(seq_here, ext_rows, model_width)
    outgoing = state_grad[:, own_bytes:].astype(jnp.bfloat16)
    handed = from_behind(outgoing, "seq", 1)
    rim_rows = handed.shape[1]
    local_part = state_grad[:, :own_bytes].at[:, :rim_rows].add(handed.astype(jnp.float32))
    byte_grad = local_part.astype(jnp.bfloat16)
    partial_value = lax.psum_scatter(
        lax.dot_general(
            flat_grads, flat_states, (((0,), (0,)), ((), ())), preferred_element_type=jnp.float32
        ),
        "seq",
        scatter_dimension=0,
        tiled=True,
    )
    partial_value = lax.psum_scatter(partial_value, "dp", scatter_dimension=1, tiled=True)
    kv_grad = partial_value.T
    return (byte_grad, query_grad, kv_grad)


NY = 2
CORES = 2
MESH = pl.DeviceIdType.MESH


def places():
    dp = lax.axis_index("dp")
    seq = lax.axis_index("seq")
    return (dp // NY, dp % NY, seq // CORES, seq % CORES)


def remote(src, dst, send, recv, dp, seq):
    return pltpu.make_async_remote_copy(
        src_ref=src,
        dst_ref=dst,
        send_sem=send,
        recv_sem=recv,
        device_id=(dp, seq),
        device_id_type=MESH,
    )


def meet(n_dp, n_seq):
    dp = lax.axis_index("dp")
    seq = lax.axis_index("seq")
    barrier = pltpu.get_barrier_semaphore()
    for step in range(1, n_dp):
        pl.semaphore_signal(
            barrier, inc=1, device_id=(lax.rem(dp + step, n_dp), seq), device_id_type=MESH
        )
    for step in range(1, n_seq):
        pl.semaphore_signal(
            barrier, inc=1, device_id=(dp, lax.rem(seq + step, n_seq)), device_id_type=MESH
        )
    pl.semaphore_wait(barrier, n_dp - 1 + n_seq - 1)


def whole_kernel(
    n_dp, n_seq, slots_all,
    w_ref, ps_hbm, pc_hbm, states_ref, pq_hbm, og_hbm,
    byte_ref, qg_ref, out_ref,
    ps_ref, pc_ref, w_all, counts, cnt_src, ext, proj, pgrad, pq_ref, og_ref, g_ref, rim, handed,
    cbuf, xout, xbuf, keep, yout, ybuf, zout, zbuf,
    l_sem, gz_send, gz_recv, gy_send, gy_recv, gx_send, gx_recv, gc_send, gc_recv,
    n_send, n_recv, h_send, h_recv,
    c_send, c_recv, x_send, x_recv, y_send, y_recv, z_send, z_recv, r_send, r_recv,
):
    z, y, x, c = places()
    n_z = n_dp // NY
    me_dp, me_seq = lax.axis_index("dp"), lax.axis_index("seq")
    x_peer, c_peer = (1 - x) * CORES + c, x * CORES + 1 - c
    far = (1 - x) * CORES + 1 - c
    y_peer = z * NY + 1 - y
    rows, model = w_ref.shape
    width = w_ref.shape[1] // n_seq
    own_bytes = states_ref.shape[0]
    reach = rim.shape[0]

    def rows_of(block):
        return pl.ds(pl.multiple_of(block * rows, rows), rows)

    def cols_of(quarter):
        return pl.ds(pl.multiple_of(quarter * width, width), width)

    loads = [
        pltpu.make_async_copy(states_ref, ext.at[pl.ds(0, own_bytes)], l_sem.at[0]),
        pltpu.make_async_copy(pq_hbm, pq_ref, l_sem.at[1]),
        pltpu.make_async_copy(og_hbm, og_ref, l_sem.at[2]),
        pltpu.make_async_copy(w_ref, w_all.at[rows_of(me_dp)], l_sem.at[3]),
        pltpu.make_async_copy(pc_hbm, pc_ref, l_sem.at[4]),
        pltpu.make_async_copy(ps_hbm, ps_ref, l_sem.at[5]),
    ]
    for k in (4, 3, 0, 1, 2, 5):
        loads[k].start()
    loads[4].wait()
    total = pc_ref[0, 0]
    for shard in range(1, n_seq):
        total = total + pc_ref[0, shard]
    cnt_src[...] = jnp.full(cnt_src.shape, total.astype(jnp.float32))
    counts[0] = cnt_src[...]
    meet(n_dp, n_seq)
    loads[3].wait()

    def part(block, quarter):
        return w_all.at[rows_of(block), cols_of(quarter)]

    def block_of(d, other):
        return lax.rem(z + d, n_z) * NY + (1 - y if other else y)

    started = []

    def go(copy):
        copy.start()
        started.append(copy)

    def arrived(dst, send, recv):
        remote(dst, dst, send, recv, me_dp, x_peer).wait_recv()

    z_order = [1, n_z - 1] + list(range(2, n_z - 1)) if n_z > 2 else list(range(1, n_z))
    if n_z == 4:
        targets = [z + 1 - 2 * lax.rem(z, 2), jnp.where(z < 2, 2, 1), jnp.where(z < 2, 3, 0)]
    else:
        targets = [lax.rem(z + d, n_z) for d in z_order]
    ahead = [lax.rem(t - z + n_z, n_z) for t in targets]
    behind = [lax.rem(z - t + n_z, n_z) for t in targets]
    own = part(me_dp, me_seq)
    for t, d in zip(targets, ahead):
        go(remote(own, own, gz_send.at[d], gz_recv.at[d], t * NY + y, me_seq))
    for side, column in enumerate((me_seq, x_peer)):
        piece = part(me_dp, column)
        go(
            remote(
                piece, piece, gy_send.at[side * n_z], gy_recv.at[side * n_z], y_peer, me_seq
            )
        )
    loads[0].wait()

    @pl.when(me_seq > 0)
    def _():
        remote(
            ext.at[pl.ds(0, reach)], ext.at[pl.ds(own_bytes, reach)], h_send, h_recv,
            me_dp, me_seq - 1,
        ).start()

    @pl.when(me_seq == n_seq - 1)
    def _():
        ext[own_bytes:, :] = jnp.zeros((reach, model), ext.dtype)

    for step in range(1, n_dp):
        go(
            remote(
                cnt_src, counts.at[step], n_send.at[step], n_recv.at[step],
                lax.rem(me_dp + step, n_dp), me_seq,
            )
        )

    def back_block(d, other):
        return block_of(n_z - d, other)

    def share(d, other, over=True):
        here = part(back_block(d, other), me_seq)
        slot = n_z * other + d
        if over:
            go(remote(here, here, gx_send.at[slot], gx_recv.at[slot], me_dp, x_peer))
        go(remote(here, here, gc_send.at[0, slot], gc_recv.at[0, slot], me_dp, c_peer))

    for k, d in enumerate(behind):
        here = part(back_block(d, 0), me_seq)
        arrived(here, gz_send.at[d], gz_recv.at[d])
        go(remote(here, here, gy_send.at[d], gy_recv.at[d], y_peer, me_seq))
        share(d, 0)
    arrived(part(y_peer, me_seq), gy_send.at[0], gy_recv.at[0])
    share(0, 1, False)
    there = part(y_peer, x_peer)
    arrived(there, gy_send.at[n_z], gy_recv.at[n_z])
    go(remote(there, there, gc_send.at[1, n_z], gc_recv.at[1, n_z], me_dp, c_peer))
    for d in behind:
        arrived(part(back_block(d, 1), me_seq), gy_send.at[d], gy_recv.at[d])
        share(d, 1)

    @pl.when(me_seq < n_seq - 1)
    def _():
        arrived(ext.at[pl.ds(own_bytes, reach)], h_send, h_recv)

    pos = me_seq
    shards = n_seq
    ext_rows = ext.shape[0]
    key_width = pq_ref.shape[1]
    pair = 2 * HD
    attn_scale = 1.0 / math.sqrt(HD)
    tile = 256

    def project(quarter):
        cols = cols_of(quarter)
        proj[:, cols] = jnp.dot(
            ext[...], w_all[:, cols], preferred_element_type=jnp.float32
        ).astype(jnp.bfloat16)

    order = [(d, other) for other in (0, 1) for d in behind]
    project(me_seq)
    for d, other in [(0, 1)] + order:
        slot = n_z * other + d
        arrived(part(back_block(d, other), c_peer), gc_send.at[0, slot], gc_recv.at[0, slot])
    project(c_peer)
    for d, other in order:
        slot = n_z * other + d
        piece = part(back_block(d, other), x_peer)
        arrived(piece, gx_send.at[slot], gx_recv.at[slot])
        go(remote(piece, piece, gc_send.at[1, slot], gc_recv.at[1, slot], me_dp, c_peer))
    project(x_peer)
    for d, other in [(0, 1)] + order:
        slot = n_z * other + d
        arrived(part(back_block(d, other), far), gc_send.at[1, slot], gc_recv.at[1, slot])
    project(far)
    for step in range(1, n_dp):
        arrived(counts.at[step], n_send.at[step], n_recv.at[step])
    for k in (1, 2, 5):
        loads[k].wait()
    loss_scale = slots_all / jnp.sum(counts[...], axis=0)[0:1, :]

    count = pc_ref[0, pos]
    starts = ps_ref[pl.ds(pos, 1), :]
    nxt = jnp.minimum(pos + 1, shards - 1)
    next_first = ps_ref[pl.ds(nxt, 1), :][:, 0:1]
    final_end = jnp.where(pos < shards - 1, own_bytes + next_first, own_bytes)
    shifted = jnp.concatenate([starts[:, 1:], starts[:, :1]], 1)
    slot_ids = lax.broadcasted_iota(jnp.int32, (1, PSLOT), 1)
    ends = jnp.where(slot_ids + 1 < count, shifted, final_end)
    ends = jnp.where(slot_ids < count, ends, 0)
    starts = jnp.concatenate([starts, starts], 1)
    ends = jnp.concatenate([ends, ends], 1)
    byte_pos = lax.broadcasted_iota(jnp.int32, (ext_rows, 2 * PSLOT), 0)
    member = (byte_pos >= starts) & (byte_pos < ends)
    same = (lax.broadcasted_iota(jnp.int32, (2 * PSLOT, pair), 0) // PSLOT) == (
        lax.broadcasted_iota(jnp.int32, (2 * PSLOT, pair), 1) // HD
    )

    def diag(block):
        both = jnp.concatenate([block, block], 0).astype(jnp.float32)
        return jnp.where(same, both, 0.0).astype(jnp.bfloat16)

    last = (((1,), (1,)), ((), ()))
    first = (((0,), (0,)), ((), ()))
    for i in range(key_width // pair):
        kc = slice(i * pair, (i + 1) * pair)
        vc = slice(key_width + i * pair, key_width + (i + 1) * pair)
        query = diag(pq_ref[:, kc])
        up = diag(og_ref[:, kc])
        keys = proj[:, kc]
        score = lax.dot_general(keys, query, last, preferred_element_type=jnp.float32)
        score = jnp.where(member, score * attn_scale, -1e30)
        peak = jnp.max(score, axis=0, keepdims=True)
        expo = jnp.where(member, jnp.exp(score - peak), 0.0)
        denom = jnp.sum(expo, axis=0, keepdims=True)
        prob = expo / jnp.where(denom > 0.0, denom, 1.0)
        prob_grad = lax.dot_general(proj[:, vc], up, last, preferred_element_type=jnp.float32)
        delta = jnp.sum(prob * prob_grad, axis=0, keepdims=True)
        score_grad = (prob * (prob_grad - delta) * attn_scale).astype(jnp.bfloat16)
        pgrad[:, kc] = (
            loss_scale * jnp.dot(score_grad, query, preferred_element_type=jnp.float32)
        ).astype(jnp.bfloat16)
        pgrad[:, vc] = (
            loss_scale
            * jnp.dot(prob.astype(jnp.bfloat16), up, preferred_element_type=jnp.float32)
        ).astype(jnp.bfloat16)
        qg = lax.dot_general(score_grad, keys, first, preferred_element_type=jnp.float32)
        qg = jnp.where(same, qg, 0.0)
        qg_ref[:, kc] = (loss_scale * (qg[:PSLOT] + qg[PSLOT:])).astype(jnp.bfloat16)

    moved = [2, 0] if n_z > 2 else [0]
    still = [d for d in z_order if d not in moved]
    for d, other in (
        [(d, 1) for d in moved]
        + [(d, 1) for d in still]
        + [(d, 0) for d in still]
        + [(d, 0) for d in moved]
    ):
        slot, block = n_z * other + d, block_of(d, other)
        g_ref[rows_of(block), :] = lax.dot_general(
            ext[:, rows_of(block)], pgrad[...], first, preferred_element_type=jnp.float32
        ).astype(jnp.bfloat16)
        for side, column in enumerate((far, c_peer)):
            go(
                remote(
                    g_ref.at[rows_of(block), cols_of(column)], cbuf.at[side, slot],
                    c_send.at[side, slot], c_recv.at[side, slot], me_dp, c_peer,
                )
            )

    def paired(side, d, other):
        slot = n_z * other + d
        arrived(cbuf.at[side, slot], c_send.at[side, slot], c_recv.at[side, slot])
        column = me_seq if side else x_peer
        mine = g_ref[rows_of(block_of(d, other)), cols_of(column)]
        return mine.astype(jnp.float32) + cbuf[side, slot].astype(jnp.float32)

    def over_y(side, d, value):
        yout[side, d] = value.astype(jnp.bfloat16)
        go(
            remote(
                yout.at[side, d], ybuf.at[side, d], y_send.at[side, d], y_recv.at[side, d],
                y_peer, me_seq,
            )
        )

    def from_y(side, d):
        arrived(ybuf.at[side, d], y_send.at[side, d], y_recv.at[side, d])
        return ybuf[side, d].astype(jnp.float32)

    def over_x(slot, value):
        xout[slot] = value.astype(jnp.bfloat16)
        go(remote(xout.at[slot], xbuf.at[slot], x_send.at[slot], x_recv.at[slot], me_dp, x_peer))

    def from_x(slot):
        arrived(xbuf.at[slot], x_send.at[slot], x_recv.at[slot])
        return keep[slot] + xbuf[slot].astype(jnp.float32)

    def over_z(d, value):
        zout[d] = value.astype(jnp.bfloat16)
        to = lax.rem(z + d, n_z) * NY + y
        go(remote(zout.at[d], zbuf.at[d], z_send.at[d], z_recv.at[d], to, me_seq))

    for d in moved:
        over_y(0, d, paired(0, d, 1))
        over_y(1, d, paired(1, d, 1))
    for other in (1, 0):
        for d in still:
            over_x(n_z * other + d, paired(0, d, other))
    for other in (1, 0):
        for d in still:
            keep[n_z * other + d] = paired(1, d, other)

    @pl.loop(0, model // tile)
    def _(n):
        cols = pl.ds(pl.multiple_of(n * tile, tile), tile)
        back = lax.dot_general(
            pgrad[...], w_all[cols, :], last, preferred_element_type=jnp.float32
        ).astype(jnp.bfloat16)
        byte_ref[:, cols] = back[:own_bytes]
        rim[:, cols] = back[own_bytes:]

    @pl.when(me_seq < n_seq - 1)
    def _():
        remote(rim, handed, r_send, r_recv, me_dp, me_seq + 1).start()

    for d in still:
        over_y(1, d, from_x(n_z + d))
    for d in moved:
        over_x(d, paired(0, d, 0) + from_y(0, d))
        keep[d] = paired(1, d, 0) + from_y(1, d)
    for d in still:
        over_z(d, from_x(d) + from_y(1, d))

    @pl.when(me_seq > 0)
    def _():
        arrived(handed, r_send, r_recv)
        byte_ref[:reach, :] = (
            byte_ref[:reach, :].astype(jnp.float32) + handed[...].astype(jnp.float32)
        ).astype(jnp.bfloat16)

    done = None
    for d in moved:
        value = from_x(d)
        if d:
            over_z(d, value)
        else:
            done = value
    for d in z_order:
        arrived(zbuf.at[d], z_send.at[d], z_recv.at[d])
        done = done + zbuf[d].astype(jnp.float32)
    out_ref[...] = done

    @pl.when(me_seq > 0)
    def _():
        remote(
            ext.at[pl.ds(0, reach)], ext.at[pl.ds(own_bytes, reach)], h_send, h_recv,
            me_dp, me_seq - 1,
        ).wait_send()

    @pl.when(me_seq < n_seq - 1)
    def _():
        remote(rim, handed, r_send, r_recv, me_dp, me_seq + 1).wait_send()

    for copy in started:
        copy.wait_send()


def kernel_body(byte_states, kv_weight, patch_query, out_grad, patch_start, patch_count):
    n_dp, n_seq = lax.axis_size("dp"), lax.axis_size("seq")
    n_z = n_dp // NY
    model = byte_states.shape[2]
    own_bytes = byte_states.shape[1]
    rows, cols = kv_weight.shape
    width = cols // n_seq
    key_width = patch_query.shape[2]
    ext_rows = own_bytes + REACH
    vmem = pl.BlockSpec(memory_space=pltpu.VMEM)
    hbm = pl.BlockSpec(memory_space=pltpu.HBM)
    half = jnp.bfloat16

    def buf(*shape, dtype=half):
        return pltpu.VMEM(shape, dtype)

    def sems(*shape):
        return [pltpu.SemaphoreType.DMA(shape)] * 2

    byte_grad, query_grad, kv_grad = pl.pallas_call(
        functools.partial(whole_kernel, n_dp, n_seq, float(n_dp * n_seq * PSLOT)),
        out_shape=(
            jax.ShapeDtypeStruct((own_bytes, model), half),
            jax.ShapeDtypeStruct((PSLOT, key_width), half),
            jax.ShapeDtypeStruct((rows, width), jnp.float32),
        ),
        in_specs=[hbm] * 6,
        out_specs=(vmem, vmem, vmem),
        scratch_shapes=[
            pltpu.VMEM(patch_start.shape[1:], jnp.int32),
            pltpu.SMEM(patch_count.shape, jnp.int32),
            buf(model, cols),
            buf(n_dp, 8, 128, dtype=jnp.float32),
            buf(8, 128, dtype=jnp.float32),
            buf(ext_rows, model),
            buf(ext_rows, cols),
            buf(ext_rows, cols),
            buf(PSLOT, key_width),
            buf(PSLOT, key_width),
            buf(model, cols),
            buf(REACH, model),
            buf(REACH, model),
            buf(2, n_dp, rows, width),
            buf(n_dp, rows, width),
            buf(n_dp, rows, width),
            buf(n_dp, rows, width, dtype=jnp.float32),
            buf(2, n_z, rows, width),
            buf(2, n_z, rows, width),
            buf(n_z, rows, width),
            buf(n_z, rows, width),
            pltpu.SemaphoreType.DMA((6,)),
            *sems(n_z), *sems(2 * n_z), *sems(n_dp), *sems(2, n_dp),
            *sems(n_dp), *sems(),
            *sems(2, n_dp), *sems(n_dp), *sems(2, n_z), *sems(n_z), *sems(),
        ],
        compiler_params=pltpu.CompilerParams(
            collective_id=0, has_side_effects=True, vmem_limit_bytes=63 * 1024 * 1024
        ),
        name="whole",
    )(
        kv_weight, patch_start[0], patch_count, byte_states[0], patch_query[0], out_grad[0]
    )
    return (byte_grad[None], query_grad[None], kv_grad)


def body(byte_states, kv_weight, patch_query, out_grad, patch_start, patch_count):
    n_dp, n_seq = lax.axis_size("dp"), lax.axis_size("seq")
    fits = (
        n_seq == 2 * CORES
        and n_dp % NY == 0
        and n_dp <= 16
        and byte_states.shape[0] == 1
        and kv_weight.shape[1] % (128 * n_seq) == 0
    )
    chosen = kernel_body if fits else plain_body
    return chosen(byte_states, kv_weight, patch_query, out_grad, patch_start, patch_count)


def solution(mesh):
    in_specs = (
        P("dp", "seq", None),
        P("dp", None),
        P("dp", "seq", None),
        P("dp", "seq", None),
        P("dp", None, None),
        P("dp", None),
    )
    out_specs = (P("dp", "seq", None), P("dp", "seq", None), P("dp", "seq"))
    return jax.shard_map(body, mesh=mesh, in_specs=in_specs, out_specs=out_specs, check_vma=False)
```

profile of v0, /device:TPU:1, one launch (start us, length us, event | category | flops | bytes accessed | tf_op | source)
XLA Modules:
  0.0 48.6 jit_solution(8425020485256048524)
XLA Ops:
  0.6 44.5 %whole.1 = (bf16[256,1024]{1,0:T(8,128)(2,1)}, bf16[64,512]{1,0:T(8,128)(2,1)}, f32[128,256]{1,0:T(8,128)}) custom-call(bf16[128,1024]{1,0:T(8,128)(2,1)} %w_ref.1, s32[4,64]{1,0:T(4,128)} %bitcast.11, s32[1,4]{1,0:T(1,128)} %pc_hbm.1, bf16[256,1024]{1,0:T(8,128)(2,1)} %bitcast.6, bf16[64,512]{1,0:T(8,128)(2,1)} %bitcast.8, bf16[64,512]{1,0:T(8,128)(2,1)} %bitcast.9), custom_call_target="tpu_custom_call" | custom-call | tf_op jit(solution)/shard_map/whole/pallas_call | solution.py:506
  45.1 0.0 copy-start.1
  45.1 1.9 %copy.12 = bf16[1,256,1024]{2,1,0:T(8,128)(2,1)} copy(bf16[1,256,1024]{2,1,0:T(8,128)(2,1)} %bitcast.7) | data formatting | bytes 1048576
  47.0 0.0 copy-done.1
  47.0 0.0 copy-start
  47.0 0.6 %copy.13 = bf16[1,64,512]{2,1,0:T(8,128)(2,1)} copy(bf16[1,64,512]{2,1,0:T(8,128)(2,1)S(1)} %bitcast.10) | data formatting | bytes 131072
  47.6 0.3 copy-done
  47.9 0.7 %copy.14 = f32[128,256]{1,0:T(8,128)} copy(f32[128,256]{1,0:T(8,128)S(1)} %copy-done) | data formatting | bytes 262144
Async XLA Ops:
  45.1 1.9 %copy-start.1 = (bf16[64,512]{1,0:T(8,128)(2,1)S(1)}, bf16[64,512]{1,0:T(8,128)(2,1)}, u32[]{:S(2)}) copy-start(bf16[64,512]{1,0:T(8,128)(2,1)} %get-tuple-element.7) | copy-start | bytes 196612
  47.0 0.9 %copy-start = (f32[128,256]{1,0:T(8,128)S(1)}, f32[128,256]{1,0:T(8,128)}, u32[]{:S(2)}) copy-start(f32[128,256]{1,0:T(8,128)} %get-tuple-element.14) | copy-start | bytes 393220
where the time goes:
time: 49.6 us; the launch traced here: 48.6 us
  Pallas kernels  44.5 us (90%)
  local copies, waits for them, and re-layouts  3.49 us (7%)
  between operations  0.65 us (1%)
    pallas_call x1, Pallas kernels, kernel_body(): pl.pallas_call(functools.partial(whole_kernel, n_dp, n_seq, float(n_dp *...  44.5 us
    unnamed x7, local copies, waits for them, and re-layouts  3.49 us

commit v1 on v0

--- a/solution.py
+++ b/solution.py
@@ -139,9 +139,20 @@
     )
 
 
+def flipped(value, mask):
+    bit = 1
+    while bit <= mask:
+        if mask & bit:
+            value = value + bit * (1 - 2 * ((value // bit) % 2))
+        bit *= 2
+    return value
+
+
 def meet(n_dp, n_seq):
     dp = lax.axis_index("dp")
     seq = lax.axis_index("seq")
+    z, y, x, c = places()
+    n_z = n_dp // NY
     barrier = pltpu.get_barrier_semaphore()
     for step in range(1, n_dp):
         pl.semaphore_signal(
@@ -151,25 +162,34 @@
         pl.semaphore_signal(
             barrier, inc=1, device_id=(dp, lax.rem(seq + step, n_seq)), device_id_type=MESH
         )
-    pl.semaphore_wait(barrier, n_dp - 1 + n_seq - 1)
+    for mask in range(1, n_z):
+        pl.semaphore_signal(
+            barrier,
+            inc=1,
+            device_id=(flipped(z, mask) * NY + y, x * CORES + 1 - c),
+            device_id_type=MESH,
+        )
+    pl.semaphore_wait(barrier, n_dp - 1 + n_seq - 1 + n_z - 1)
 
 
 def whole_kernel(
     n_dp, n_seq, slots_all,
     w_ref, ps_hbm, pc_hbm, states_ref, pq_hbm, og_hbm,
     byte_ref, qg_ref, out_ref,
-    ps_ref, pc_ref, w_all, counts, cnt_src, ext, proj, pgrad, pq_ref, og_ref, g_ref, rim, handed,
-    cbuf, xout, xbuf, keep, yout, ybuf, zout, zbuf,
+    ps_ref, pc_ref, w_all, counts, cnt_src, ext, ext_t, proj, pgrad, split, pq_ref, og_ref,
+    g_send, g_keep, g_buf, rim, handed,
+    a_out, a_buf, hold, b_out, b_buf, z_out, z_buf, s_out, s_buf,
     l_sem, gz_send, gz_recv, gy_send, gy_recv, gx_send, gx_recv, gc_send, gc_recv,
     n_send, n_recv, h_send, h_recv,
-    c_send, c_recv, x_send, x_recv, y_send, y_recv, z_send, z_recv, r_send, r_recv,
+    c_send, c_recv, a_send, a_recv, b_send, b_recv, z_send, z_recv, s_send, s_recv, r_send, r_recv,
 ):
     z, y, x, c = places()
     n_z = n_dp // NY
     me_dp, me_seq = lax.axis_index("dp"), lax.axis_index("seq")
     x_peer, c_peer = (1 - x) * CORES + c, x * CORES + 1 - c
-    far = (1 - x) * CORES + 1 - c
     y_peer = z * NY + 1 - y
+    q_own, q_core = x + CORES * c, x + CORES * (1 - c)
+    q_over, q_far = 1 - x + CORES * c, 1 - x + CORES * (1 - c)
     rows, model = w_ref.shape
     width = w_ref.shape[1] // n_seq
     own_bytes = states_ref.shape[0]
@@ -222,10 +242,10 @@
         targets = [lax.rem(z + d, n_z) for d in z_order]
     ahead = [lax.rem(t - z + n_z, n_z) for t in targets]
     behind = [lax.rem(z - t + n_z, n_z) for t in targets]
-    own = part(me_dp, me_seq)
+    own = part(me_dp, q_own)
     for t, d in zip(targets, ahead):
         go(remote(own, own, gz_send.at[d], gz_recv.at[d], t * NY + y, me_seq))
-    for side, column in enumerate((me_seq, x_peer)):
+    for side, column in enumerate((q_own, q_over)):
         piece = part(me_dp, column)
         go(
             remote(
@@ -253,28 +273,30 @@
             )
         )
 
+    ext_t[:, :own_bytes] = ext[:own_bytes, :].T
+
     def back_block(d, other):
         return block_of(n_z - d, other)
 
     def share(d, other, over=True):
-        here = part(back_block(d, other), me_seq)
+        here = part(back_block(d, other), q_own)
         slot = n_z * other + d
         if over:
             go(remote(here, here, gx_send.at[slot], gx_recv.at[slot], me_dp, x_peer))
         go(remote(here, here, gc_send.at[0, slot], gc_recv.at[0, slot], me_dp, c_peer))
 
     for k, d in enumerate(behind):
-        here = part(back_block(d, 0), me_seq)
+        here = part(back_block(d, 0), q_own)
         arrived(here, gz_send.at[d], gz_recv.at[d])
         go(remote(here, here, gy_send.at[d], gy_recv.at[d], y_peer, me_seq))
         share(d, 0)
-    arrived(part(y_peer, me_seq), gy_send.at[0], gy_recv.at[0])
+    arrived(part(y_peer, q_own), gy_send.at[0], gy_recv.at[0])
     share(0, 1, False)
-    there = part(y_peer, x_peer)
+    there = part(y_peer, q_over)
     arrived(there, gy_send.at[n_z], gy_recv.at[n_z])
     go(remote(there, there, gc_send.at[1, n_z], gc_recv.at[1, n_z], me_dp, c_peer))
     for d in behind:
-        arrived(part(back_block(d, 1), me_seq), gy_send.at[d], gy_recv.at[d])
+        arrived(part(back_block(d, 1), q_own), gy_send.at[d], gy_recv.at[d])
         share(d, 1)
 
     @pl.when(me_seq < n_seq - 1)
@@ -285,9 +307,11 @@
     shards = n_seq
     ext_rows = ext.shape[0]
     key_width = pq_ref.shape[1]
-    pair = 2 * HD
+    half = width // 2
     attn_scale = 1.0 / math.sqrt(HD)
     tile = 256
+    last = (((1,), (1,)), ((), ()))
+    first = (((0,), (0,)), ((), ()))
 
     def project(quarter):
         cols = cols_of(quarter)
@@ -296,26 +320,13 @@
         ).astype(jnp.bfloat16)
 
     order = [(d, other) for other in (0, 1) for d in behind]
-    project(me_seq)
-    for d, other in [(0, 1)] + order:
-        slot = n_z * other + d
-        arrived(part(back_block(d, other), c_peer), gc_send.at[0, slot], gc_recv.at[0, slot])
-    project(c_peer)
-    for d, other in order:
-        slot = n_z * other + d
-        piece = part(back_block(d, other), x_peer)
-        arrived(piece, gx_send.at[slot], gx_recv.at[slot])
-        go(remote(piece, piece, gc_send.at[1, slot], gc_recv.at[1, slot], me_dp, c_peer))
-    project(x_peer)
-    for d, other in [(0, 1)] + order:
-        slot = n_z * other + d
-        arrived(part(back_block(d, other), far), gc_send.at[1, slot], gc_recv.at[1, slot])
-    project(far)
+    project(q_own)
+    ext_t[:, own_bytes:] = ext[own_bytes:, :].T
     for step in range(1, n_dp):
         arrived(counts.at[step], n_send.at[step], n_recv.at[step])
     for k in (1, 2, 5):
         loads[k].wait()
-    loss_scale = slots_all / jnp.sum(counts[...], axis=0)[0:1, :]
+    loss_scale = slots_all / jnp.sum(counts[...], axis=0)[0:1, 0:1]
 
     count = pc_ref[0, pos]
     starts = ps_ref[pl.ds(pos, 1), :]
@@ -326,23 +337,30 @@
     slot_ids = lax.broadcasted_iota(jnp.int32, (1, PSLOT), 1)
     ends = jnp.where(slot_ids + 1 < count, shifted, final_end)
     ends = jnp.where(slot_ids < count, ends, 0)
-    starts = jnp.concatenate([starts, starts], 1)
-    ends = jnp.concatenate([ends, ends], 1)
-    byte_pos = lax.broadcasted_iota(jnp.int32, (ext_rows, 2 * PSLOT), 0)
+    heads = width // HD
+    slots = heads * PSLOT
+    starts = jnp.concatenate([starts] * heads, 1)
+    ends = jnp.concatenate([ends] * heads, 1)
+    byte_pos = lax.broadcasted_iota(jnp.int32, (ext_rows, slots), 0)
     member = (byte_pos >= starts) & (byte_pos < ends)
-    same = (lax.broadcasted_iota(jnp.int32, (2 * PSLOT, pair), 0) // PSLOT) == (
-        lax.broadcasted_iota(jnp.int32, (2 * PSLOT, pair), 1) // HD
+    same = (lax.broadcasted_iota(jnp.int32, (slots, width), 0) // PSLOT) == (
+        lax.broadcasted_iota(jnp.int32, (slots, width), 1) // HD
     )
 
     def diag(block):
-        both = jnp.concatenate([block, block], 0).astype(jnp.float32)
-        return jnp.where(same, both, 0.0).astype(jnp.bfloat16)
-
-    last = (((1,), (1,)), ((), ()))
-    first = (((0,), (0,)), ((), ()))
-    for i in range(key_width // pair):
-        kc = slice(i * pair, (i + 1) * pair)
-        vc = slice(key_width + i * pair, key_width + (i + 1) * pair)
+        every = jnp.concatenate([block] * heads, 0).astype(jnp.float32)
+        return jnp.where(same, every, 0.0).astype(jnp.bfloat16)
+
+    def lanes(index):
+        return pl.ds(pl.multiple_of(index * half, half), half)
+
+    def divide(stage, kind, value):
+        for side in (0, 1):
+            place = 2 * (1 - c - side + 2 * c * side) + kind + x - 2 * kind * x
+            split[stage, :, lanes(place)] = value[:, side * half : (side + 1) * half]
+
+    def attend(stage, group):
+        kc, vc = cols_of(group), cols_of(group + CORES)
         query = diag(pq_ref[:, kc])
         up = diag(og_ref[:, kc])
         keys = proj[:, kc]
@@ -355,100 +373,151 @@
         prob_grad = lax.dot_general(proj[:, vc], up, last, preferred_element_type=jnp.float32)
         delta = jnp.sum(prob * prob_grad, axis=0, keepdims=True)
         score_grad = (prob * (prob_grad - delta) * attn_scale).astype(jnp.bfloat16)
-        pgrad[:, kc] = (
+        key_grad = (
             loss_scale * jnp.dot(score_grad, query, preferred_element_type=jnp.float32)
         ).astype(jnp.bfloat16)
-        pgrad[:, vc] = (
+        value_grad = (
             loss_scale
             * jnp.dot(prob.astype(jnp.bfloat16), up, preferred_element_type=jnp.float32)
         ).astype(jnp.bfloat16)
+        pgrad[:, kc] = key_grad
+        pgrad[:, vc] = value_grad
+        divide(stage, 0, key_grad)
+        divide(stage, 1, value_grad)
         qg = lax.dot_general(score_grad, keys, first, preferred_element_type=jnp.float32)
         qg = jnp.where(same, qg, 0.0)
-        qg_ref[:, kc] = (loss_scale * (qg[:PSLOT] + qg[PSLOT:])).astype(jnp.bfloat16)
-
-    moved = [2, 0] if n_z > 2 else [0]
-    still = [d for d in z_order if d not in moved]
-    for d, other in (
-        [(d, 1) for d in moved]
-        + [(d, 1) for d in still]
-        + [(d, 0) for d in still]
-        + [(d, 0) for d in moved]
-    ):
-        slot, block = n_z * other + d, block_of(d, other)
-        g_ref[rows_of(block), :] = lax.dot_general(
-            ext[:, rows_of(block)], pgrad[...], first, preferred_element_type=jnp.float32
+        qg = sum(qg[h * PSLOT : (h + 1) * PSLOT] for h in range(heads))
+        qg_ref[:, kc] = (loss_scale * qg).astype(jnp.bfloat16)
+
+    masks = [mask for mask in (2, 3) if mask < n_z] + [1] if n_z > 1 else []
+    masks = masks + list(range(4, n_z)) + [0]
+    both = NY * rows
+
+    def rows_at(mask):
+        return pl.ds(pl.multiple_of(flipped(z, mask) * both, both), both)
+
+    def weight_terms(stage):
+        g_send[stage] = jnp.dot(
+            ext_t[...], split[stage, :, :width], preferred_element_type=jnp.float32
         ).astype(jnp.bfloat16)
-        for side, column in enumerate((far, c_peer)):
+        for mask in masks:
+            there = rows_at(mask)
             go(
                 remote(
-                    g_ref.at[rows_of(block), cols_of(column)], cbuf.at[side, slot],
-                    c_send.at[side, slot], c_recv.at[side, slot], me_dp, c_peer,
+                    g_send.at[stage, there], g_buf.at[stage, there],
+                    c_send.at[stage, mask], c_recv.at[stage, mask], me_dp, c_peer,
                 )
             )
-
-    def paired(side, d, other):
+        g_keep[stage] = jnp.dot(
+            ext_t[...], split[stage, :, width:], preferred_element_type=jnp.float32
+        )
+
+    a_dev = (me_dp * (1 - c) + y_peer * c, x_peer * (1 - c) + me_seq * c)
+    b_dev = (y_peer * (1 - c) + me_dp * c, me_seq * (1 - c) + x_peer * c)
+
+    def paired(stage, mask, one, two):
+        across, other = one * (1 - c) + two * c, one * c + two * (1 - c)
+        here = rows_of(flipped(z, mask) * NY + y + other * (1 - 2 * y))
+        cols = lanes(across)
+        return g_keep[stage, here, cols] + g_buf[stage, here, cols].astype(jnp.float32)
+
+    def step_a(stage):
+        twin = stage * c + (1 - stage) * (1 - c)
+        for mask in masks:
+            there = g_buf.at[stage, rows_at(mask)]
+            arrived(there, c_send.at[stage, mask], c_recv.at[stage, mask])
+            for two in (0, 1):
+                a_out[stage, mask, two * rows : (two + 1) * rows] = paired(
+                    stage, mask, 1, two
+                ).astype(jnp.bfloat16)
+            go(
+                remote(
+                    a_out.at[stage, mask], a_buf.at[twin, mask],
+                    a_send.at[stage, mask], a_recv.at[twin, mask], *a_dev,
+                )
+            )
+
+    def step_b(stage):
+        twin = stage * (1 - c) + (1 - stage) * c
+        for mask in masks:
+            arrived(a_buf.at[stage, mask], a_send.at[stage, mask], a_recv.at[stage, mask])
+            b_out[stage, mask] = (
+                paired(stage, mask, 0, 1) + a_buf[stage, mask, rows:].astype(jnp.float32)
+            ).astype(jnp.bfloat16)
+            go(
+                remote(
+                    b_out.at[stage, mask], b_buf.at[twin, mask],
+                    b_send.at[stage, mask], b_recv.at[twin, mask], *b_dev,
+                )
+            )
+            hold[stage, mask] = paired(stage, mask, 0, 0) + a_buf[stage, mask, :rows].astype(
+                jnp.float32
+            )
+
+    def step_z(stage, group):
+        for mask in masks:
+            arrived(b_buf.at[stage, mask], b_send.at[stage, mask], b_recv.at[stage, mask])
+            value = hold[stage, mask] + b_buf[stage, mask].astype(jnp.float32)
+            if mask:
+                z_out[stage, mask] = value.astype(jnp.bfloat16)
+                go(
+                    remote(
+                        z_out.at[stage, mask], z_buf.at[c, mask],
+                        z_send.at[stage, mask], z_recv.at[c, mask],
+                        flipped(z, mask) * NY + y, x * CORES + group,
+                    )
+                )
+                continue
+
+            @pl.when(c == group)
+            def _():
+                out_ref[:, lanes(c)] = value
+
+            @pl.when(c != group)
+            def _():
+                s_out[...] = value.astype(jnp.bfloat16)
+                remote(s_out, s_buf, s_send, s_recv, me_dp, c_peer).start()
+
+    def back(lo, hi):
+        @pl.loop(lo, hi)
+        def _(n):
+            cols = pl.ds(pl.multiple_of(n * tile, tile), tile)
+            value = lax.dot_general(
+                pgrad[...], w_all[cols, :], last, preferred_element_type=jnp.float32
+            ).astype(jnp.bfloat16)
+            byte_ref[:, cols] = value[:own_bytes]
+            rim[:, cols] = value[own_bytes:]
+
+    for d, other in [(0, 1)] + order:
         slot = n_z * other + d
-        arrived(cbuf.at[side, slot], c_send.at[side, slot], c_recv.at[side, slot])
-        column = me_seq if side else x_peer
-        mine = g_ref[rows_of(block_of(d, other)), cols_of(column)]
-        return mine.astype(jnp.float32) + cbuf[side, slot].astype(jnp.float32)
-
-    def over_y(side, d, value):
-        yout[side, d] = value.astype(jnp.bfloat16)
-        go(
-            remote(
-                yout.at[side, d], ybuf.at[side, d], y_send.at[side, d], y_recv.at[side, d],
-                y_peer, me_seq,
-            )
-        )
-
-    def from_y(side, d):
-        arrived(ybuf.at[side, d], y_send.at[side, d], y_recv.at[side, d])
-        return ybuf[side, d].astype(jnp.float32)
-
-    def over_x(slot, value):
-        xout[slot] = value.astype(jnp.bfloat16)
-        go(remote(xout.at[slot], xbuf.at[slot], x_send.at[slot], x_recv.at[slot], me_dp, x_peer))
-
-    def from_x(slot):
-        arrived(xbuf.at[slot], x_send.at[slot], x_recv.at[slot])
-        return keep[slot] + xbuf[slot].astype(jnp.float32)
-
-    def over_z(d, value):
-        zout[d] = value.astype(jnp.bfloat16)
-        to = lax.rem(z + d, n_z) * NY + y
-        go(remote(zout.at[d], zbuf.at[d], z_send.at[d], z_recv.at[d], to, me_seq))
-
-    for d in moved:
-        over_y(0, d, paired(0, d, 1))
-        over_y(1, d, paired(1, d, 1))
-    for other in (1, 0):
-        for d in still:
-            over_x(n_z * other + d, paired(0, d, other))
-    for other in (1, 0):
-        for d in still:
-            keep[n_z * other + d] = paired(1, d, other)
-
-    @pl.loop(0, model // tile)
-    def _(n):
-        cols = pl.ds(pl.multiple_of(n * tile, tile), tile)
-        back = lax.dot_general(
-            pgrad[...], w_all[cols, :], last, preferred_element_type=jnp.float32
-        ).astype(jnp.bfloat16)
-        byte_ref[:, cols] = back[:own_bytes]
-        rim[:, cols] = back[own_bytes:]
+        arrived(part(back_block(d, other), q_core), gc_send.at[0, slot], gc_recv.at[0, slot])
+    project(q_core)
+    attend(0, x)
+    weight_terms(0)
+    for d, other in order:
+        slot = n_z * other + d
+        piece = part(back_block(d, other), q_over)
+        arrived(piece, gx_send.at[slot], gx_recv.at[slot])
+        go(remote(piece, piece, gc_send.at[1, slot], gc_recv.at[1, slot], me_dp, c_peer))
+    step_a(0)
+    project(q_over)
+    for d, other in [(0, 1)] + order:
+        slot = n_z * other + d
+        arrived(part(back_block(d, other), q_far), gc_send.at[1, slot], gc_recv.at[1, slot])
+    project(q_far)
+    attend(1, 1 - x)
+    weight_terms(1)
+    step_a(1)
+    step_b(1 - c)
+    back(0, model // tile)
 
     @pl.when(me_seq < n_seq - 1)
     def _():
         remote(rim, handed, r_send, r_recv, me_dp, me_seq + 1).start()
 
-    for d in still:
-        over_y(1, d, from_x(n_z + d))
-    for d in moved:
-        over_x(d, paired(0, d, 0) + from_y(0, d))
-        keep[d] = paired(1, d, 0) + from_y(1, d)
-    for d in still:
-        over_z(d, from_x(d) + from_y(1, d))
+    step_b(c)
+    step_z(1, 1 - x)
+    step_z(0, x)
 
     @pl.when(me_seq > 0)
     def _():
@@ -457,17 +526,14 @@
             byte_ref[:reach, :].astype(jnp.float32) + handed[...].astype(jnp.float32)
         ).astype(jnp.bfloat16)
 
-    done = None
-    for d in moved:
-        value = from_x(d)
-        if d:
-            over_z(d, value)
-        else:
-            done = value
-    for d in z_order:
-        arrived(zbuf.at[d], z_send.at[d], z_recv.at[d])
-        done = done + zbuf[d].astype(jnp.float32)
-    out_ref[...] = done
+    arrived(s_buf, s_send, s_recv)
+    for side, core in enumerate((c, 1 - c)):
+        done = s_buf[...].astype(jnp.float32) if side else out_ref[:, lanes(c)]
+        for mask in masks[:-1]:
+            arrived(z_buf.at[core, mask], z_send.at[0, mask], z_recv.at[core, mask])
+            done = done + z_buf[core, mask].astype(jnp.float32)
+        out_ref[:, lanes(core)] = done
+    remote(s_out, s_buf, s_send, s_recv, me_dp, c_peer).wait_send()
 
     @pl.when(me_seq > 0)
     def _():
@@ -482,6 +548,17 @@
 
     for copy in started:
         copy.wait_send()
+
+
+def hand_out(a_in, b_in, c_in, a_out, b_out, c_out, sem):
+    copies = [
+        pltpu.make_async_copy(src, dst, sem.at[k])
+        for k, (src, dst) in enumerate(((a_in, a_out), (b_in, b_out), (c_in, c_out)))
+    ]
+    for copy in copies:
+        copy.start()
+    for copy in copies:
+        copy.wait()
 
 
 def kernel_body(byte_states, kv_weight, patch_query, out_grad, patch_start, patch_count):
@@ -506,9 +583,9 @@
     byte_grad, query_grad, kv_grad = pl.pallas_call(
         functools.partial(whole_kernel, n_dp, n_seq, float(n_dp * n_seq * PSLOT)),
         out_shape=(
-            jax.ShapeDtypeStruct((own_bytes, model), half),
-            jax.ShapeDtypeStruct((PSLOT, key_width), half),
-            jax.ShapeDtypeStruct((rows, width), jnp.float32),
+            pltpu.VMEM((own_bytes, model), half),
+            pltpu.VMEM((PSLOT, key_width), half),
+            pltpu.VMEM((rows, width), jnp.float32),
         ),
         in_specs=[hbm] * 6,
         out_specs=(vmem, vmem, vmem),
@@ -519,25 +596,30 @@
             buf(n_dp, 8, 128, dtype=jnp.float32),
             buf(8, 128, dtype=jnp.float32),
             buf(ext_rows, model),
+            buf(model, ext_rows),
             buf(ext_rows, cols),
             buf(ext_rows, cols),
+            buf(2, ext_rows, 2 * width),
             buf(PSLOT, key_width),
             buf(PSLOT, key_width),
-            buf(model, cols),
+            buf(2, model, width),
+            buf(2, model, width, dtype=jnp.float32),
+            buf(2, model, width),
             buf(REACH, model),
             buf(REACH, model),
-            buf(2, n_dp, rows, width),
-            buf(n_dp, rows, width),
-            buf(n_dp, rows, width),
-            buf(n_dp, rows, width, dtype=jnp.float32),
-            buf(2, n_z, rows, width),
-            buf(2, n_z, rows, width),
-            buf(n_z, rows, width),
-            buf(n_z, rows, width),
+            buf(2, n_z, NY * rows, width // 2),
+            buf(2, n_z, NY * rows, width // 2),
+            buf(2, n_z, rows, width // 2, dtype=jnp.float32),
+            buf(2, n_z, rows, width // 2),
+            buf(2, n_z, rows, width // 2),
+            buf(2, n_z, rows, width // 2),
+            buf(2, n_z, rows, width // 2),
+            buf(rows, width // 2),
+            buf(rows, width // 2),
             pltpu.SemaphoreType.DMA((6,)),
             *sems(n_z), *sems(2 * n_z), *sems(n_dp), *sems(2, n_dp),
             *sems(n_dp), *sems(),
-            *sems(2, n_dp), *sems(n_dp), *sems(2, n_z), *sems(n_z), *sems(),
+            *sems(2, n_z), *sems(2, n_z), *sems(2, n_z), *sems(2, n_z), *sems(), *sems(),
         ],
         compiler_params=pltpu.CompilerParams(
             collective_id=0, has_side_effects=True, vmem_limit_bytes=63 * 1024 * 1024
@@ -546,6 +628,19 @@
     )(
         kv_weight, patch_start[0], patch_count, byte_states[0], patch_query[0], out_grad[0]
     )
+    byte_grad, query_grad, kv_grad = pl.pallas_call(
+        hand_out,
+        out_shape=(
+            jax.ShapeDtypeStruct((own_bytes, model), half),
+            jax.ShapeDtypeStruct((PSLOT, key_width), half),
+            jax.ShapeDtypeStruct((rows, width), jnp.float32),
+        ),
+        in_specs=[pl.BlockSpec(memory_space=pl.ANY)] * 3,
+        out_specs=[hbm] * 3,
+        scratch_shapes=[pltpu.SemaphoreType.DMA((3,))],
+        compiler_params=pltpu.CompilerParams(vmem_limit_bytes=1024 * 1024),
+        name="hand_out",
+    )(byte_grad, query_grad, kv_grad)
     return (byte_grad[None], query_grad[None], kv_grad)
 
 
@@ -556,7 +651,9 @@
         and n_dp % NY == 0
         and n_dp <= 16
         and byte_states.shape[0] == 1
-        and kv_weight.shape[1] % (128 * n_seq) == 0
+        and n_dp // NY in (2, 4, 8)
+        and kv_weight.shape[1] % (256 * n_seq) == 0
+        and kv_weight.shape[1] == 2 * patch_query.shape[2]
     )
     chosen = kernel_body if fits else plain_body
     return chosen(byte_states, kv_weight, patch_query, out_grad, patch_start, patch_count)

time: 49.6 us -> 42.9 us (0.86)
  the two profiles are of different devices: /device:TPU:1 before, /device:TPU:0 now
where the time goes in v1:
time: 42.9 us; the launch traced here: 42.7 us
  Pallas kernels  42.1 us (98%)
  between operations  0.64 us (1%)
    pallas_call x1, Pallas kernels, kernel_body(): pl.pallas_call(functools.partial(whole_kernel, n_dp, n_seq, float(n_dp *...  41.2 us
    pallas_call x1, Pallas kernels, kernel_body(): pl.pallas_call(hand_out, out_shape=(jax.ShapeDtypeStruct((own_bytes, mode...  0.88 us

profile of v1, /device:TPU:0, one launch (start us, length us, event | category | flops | bytes accessed | tf_op | source)
XLA Modules:
  0.0 42.7 jit_solution(11847232059007135672)
XLA Ops:
  0.6 41.2 %whole.1 = (bf16[256,1024]{1,0:T(8,128)(2,1)S(1)}, bf16[64,512]{1,0:T(8,128)(2,1)S(1)}, f32[128,256]{1,0:T(8,128)S(1)}) custom-call(bf16[128,1024]{1,0:T(8,128)(2,1)} %w_ref.1, s32[4,64]{1,0:T(4,128)} %bitcast.9, s32[1,4]{1,0:T(1,128)} %pc_hbm.1, bf16[256,1024]{1,0:T(8,128)(2,1)} %bitcast.6, bf16[64,512]{1,0:T(8,128)(2,1)} %bitcast.7, bf16[64,512]{1,0:T(8,128)(2,1)} %bitcast.8), custom_call_target="tpu_custom_call" | custom-call | tf_op jit(solution)/shard_map/whole/pallas_call | solution.py:583
  41.9 0.9 %hand_out.1 = (bf16[256,1024]{1,0:T(8,128)(2,1)}, bf16[64,512]{1,0:T(8,128)(2,1)}, f32[128,256]{1,0:T(8,128)}) custom-call(bf16[256,1024]{1,0:T(8,128)(2,1)S(1)} %get-tuple-element.9.a_in, bf16[64,512]{1,0:T(8,128)(2,1)S(1)} %get-tuple-element.10.b_in, f32[128,256]{1,0:T(8,128)S(1)} %get-tuple-element.11.c_in), custom_call_target="tpu_custom_call" | custom-call | tf_op jit(solution)/shard_map/hand_out/pallas_call | solution.py:631
